TPU v7x, 32 devices: a whole 2x2x4 slice. The times are simulated.
32 devices in a mesh: grp: 4 (over y, x), dev: 8 (over z, core).
Axes of the slice: x: 2, y: 2, z: 4, core: 2. Of those that a mesh axis runs over, the one named last changes fastest.
Arguments:
- table: bfloat16 [8, 32768, 256], P('grp', 'dev'), may hold values from -0.75 to 0.75
- token_ids: int32 [8192], P(('grp', 'dev')), may hold values from 0 to 32767, as said below
- hidden: bfloat16 [8192, 2560], P(('grp', 'dev')), may hold values from -6 to 6
- w_proj: bfloat16 [2560, 2048], replicated, may hold values from -0.125 to 0.125
- norm_gain: float32 [256], replicated, may hold values from 0.5 to 1.5
Outputs:
- served_table: bfloat16 [8, 4, 1024, 2048], P('dev', 'grp')
- layer_inputs: bfloat16 [8192, 8, 256], P(('grp', 'dev'))
Inputs may be any that keep to these rules, and one draw needn't show every extreme that they name: `token_ids`: of the 256 tokens of one device, at most 16 have ids in any one aligned block of 1024 vocabulary rows, and exactly 16 in some block.
All inputs are finite; a program needn't handle non-finite values.
Results may differ from a plain program's by a relative error of at most 0.001.
Values may be sent and summed in bfloat16 or wider, within the bound.
A program may use at most 128 MiB of HBM per device.

v0:
```python
import math
import jax
import jax.numpy as jnp
from jax import lax
from jax.sharding import PartitionSpec as P


def lookup(all_ids, local_rows, base):
    owned = local_rows.shape[0]
    count = all_ids.shape[0]
    block = math.gcd(count, 512)
    blocks = all_ids.reshape(count // block, block)

    def one_block(ids_block):
        onehot = (ids_block[:, None] - base == jnp.arange(owned, dtype=jnp.int32)[None, :]).astype(
            jnp.bfloat16
        )
        return jnp.dot(onehot, local_rows, preferred_element_type=jnp.float32).astype(jnp.bfloat16)

    return lax.map(one_block, blocks).reshape(count, local_rows.shape[1])


def on_device(table, token_ids, hidden, w_proj, norm_gain):
    n_grp = lax.axis_size("grp")
    n_dev = lax.axis_size("dev")
    g_index = lax.axis_index("grp")
    d_index = lax.axis_index("dev")
    layer_share, vocab_share, width = table.shape
    layers = layer_share * n_grp
    tok_count = token_ids.shape[0]
    moved = lax.all_to_all(table, "grp", split_axis=1, concat_axis=0, tiled=True)
    row_count = moved.shape[1]
    served_rows = jnp.transpose(moved, (1, 0, 2)).reshape(row_count, layers * width)
    served_table = served_rows.reshape(1, 1, row_count, layers * width)
    peers = n_grp * n_dev
    capacity = max(2, 2 * tok_count // peers)
    owner_block = token_ids // row_count
    owner_peer = owner_block % n_grp * n_dev + owner_block // n_grp
    positions = jnp.arange(tok_count, dtype=jnp.int32)
    same_peer = owner_peer[:, None] == owner_peer[None, :]
    earlier = positions[None, :] < positions[:, None]
    slot_index = jnp.sum((same_peer & earlier).astype(jnp.int32), axis=1)
    wanted = owner_peer * capacity + slot_index
    slot_hit = (wanted[:, None] == jnp.arange(peers * capacity, dtype=jnp.int32)[None, :]).astype(
        jnp.int32
    )
    outgoing = jnp.sum(slot_hit * (token_ids + 1)[:, None], axis=0) - 1
    base = (d_index * n_grp + g_index) * row_count
    incoming = lax.all_to_all(
        outgoing.reshape(peers, capacity), ("grp", "dev"), split_axis=0, concat_axis=0, tiled=True
    )
    found = lookup(incoming.reshape(peers * capacity), served_rows, base)
    found = found.reshape(peers, capacity, layers * width)
    replies = lax.all_to_all(found, ("grp", "dev"), split_axis=0, concat_axis=0, tiled=True)
    picker = slot_hit.astype(jnp.bfloat16)
    emb = jnp.dot(
        picker,
        replies.reshape(peers * capacity, layers * width),
        preferred_element_type=jnp.float32,
    )
    proj = jnp.dot(hidden, w_proj, preferred_element_type=jnp.float32).reshape(
        tok_count, layers, width
    )
    mean_sq = jnp.mean(proj * proj, axis=-1, keepdims=True)
    normed = proj / jnp.sqrt(mean_sq + 1e-06) * norm_gain
    emb = emb.reshape(tok_count, layers, width)
    layer_inputs = ((normed + math.sqrt(width) * emb) / math.sqrt(2.0)).astype(jnp.bfloat16)
    return (served_table, layer_inputs)


def solution(mesh):
    in_specs = (P("grp", "dev", None), P(("grp", "dev")), P(("grp", "dev"), None), P(), P())
    out_specs = (P("dev", "grp", None, None), P(("grp", "dev"), None, None))
    return jax.shard_map(
        on_device, mesh=mesh, in_specs=in_specs, out_specs=out_specs, check_vma=False
    )
```

profile of v0, /device:TPU:0, one launch (start us, length us, event | category | flops | bytes accessed | tf_op | source)
XLA Modules:
  0.0 152.2 jit_solution(1475072987152448503)
XLA Ops:
  0.6 0.8 fusion.10
  1.4 0.2 convert_reduce_fusion
  1.6 0.2 select_reduce_fusion
  1.8 0.7 sub.35
  2.5 7.3 %all-to-all-start.1 = ((s32[32,1,16]{2,1,0:T(1,128)}), s32[32,1,16]{2,1,0:T(1,128)S(1)}, u32[]{:S(2)}, u32[]{:S(2)}) async-start(s32[32,1,16]{2,1,0:T(1,128)} %bitcast.6), calls=%async_computation.1 | async-start | bytes 32768 | tf_op jit(solution)/shard_map/all_to_all | solution.py:49
  9.8 10.1 %copy.49 = bf16[2,4096,256]{2,0,1:T(2,128)(2,1)} copy(bf16[2,4096,256]{2,1,0:T(8,128)(2,1)} %param.5) | data formatting | bytes 8388608 | tf_op args[0]
  19.9 4.9 %all-to-all-start = ((bf16[2,4096,256]{2,0,1:T(2,128)(2,1)}), bf16[2,4096,256]{2,0,1:T(2,128)(2,1)}, u32[]{:S(2)}, u32[]{:S(2)}) async-start(bf16[2,4096,256]{2,0,1:T(2,128)(2,1)} %copy.49), calls=%async_computation | async-start | bytes 8388608 | tf_op jit(solution)/shard_map/all_to_all | solution.py:31
  24.9 0.1 sub.38
  24.9 48.0 %all-to-all-done = bf16[2,4096,256]{2,0,1:T(2,128)(2,1)} async-done(((bf16[2,4096,256]{2,0,1:T(2,128)(2,1)}), bf16[2,4096,256]{2,0,1:T(2,128)(2,1)}, u32[]{:S(2)}, u32[]{:S(2)}) %all-to-all-start) | async-done | bytes 4194336 | tf_op jit(solution)/shard_map/all_to_all | solution.py:31
  72.9 2.7 %copy.50 = bf16[2,4096,256]{2,1,0:T(8,128)(2,1)S(1)} copy(bf16[2,4096,256]{2,0,1:T(2,128)(2,1)} %all-to-all-done) | data formatting | bytes 8388608 | tf_op jit(solution)/shard_map/all_to_all | solution.py:31
  75.6 2.3 %copy.51 = bf16[4,2,1024,256]{3,2,1,0:T(8,128)(2,1)} copy(bf16[4,2,1024,256]{3,2,0,1:T(8,128)(2,1)S(1)} %bitcast.36) | data formatting | bytes 8388608 | tf_op jit(solution)/shard_map/all_to_all | solution.py:31
  77.9 6.4 %copy.52 = bf16[1024,8,256]{0,2,1:T(8,128)(2,1)} copy(bf16[1024,8,256]{2,0,1:T(8,128)(2,1)} %bitcast.37) | data formatting | bytes 8388608 | tf_op jit(solution)/shard_map/transpose | solution.py:33
  84.4 5.9 %convolution_convert_fusion = bf16[512,2048]{1,0:T(8,128)(2,1)} fusion(bf16[1024,2048]{0,1:T(8,128)(2,1)} %bitcast.34, s32[512]{0:T(512)S(1)} %sub.38), kind=kOutput, calls=%fused_computation | convolution fusion | flops 2149056512 | bytes 6293504 | tf_op jit(solution)/shard_map/while/body/eval_jaxpr/dot_general | solution.py:18
  90.3 4.8 %all-to-all-start.2 = ((bf16[32,16,2048]{2,1,0:T(8,128)(2,1)}), bf16[32,16,2048]{2,1,0:T(8,128)(2,1)S(1)}, u32[]{:S(2)}, u32[]{:S(2)}) async-start(bf16[32,16,2048]{2,1,0:T(8,128)(2,1)} %bitcast.42), calls=%async_computation.2 | async-start | bytes 4194304 | tf_op jit(solution)/shard_map/all_to_all | solution.py:54
  95.1 5.6 %fusion.11 = f32[256,2048]{1,0:T(8,128)S(1)} fusion(bf16[256,2560]{1,0:T(8,128)(2,1)S(1)} %copy-done, bf16[2560,2048]{1,0:T(8,128)(2,1)} %param.8), kind=kOutput, calls=%fused_computation.33 | convolution fusion | flops 2684354560 | bytes 13893632 | tf_op jit(solution)/shard_map/dot_general | solution.py:61
  100.7 0.9 copy.61
  101.6 0.5 copy-done.1
  102.1 0.3 multiply_reduce_fusion
  102.4 0.1 copy.53
  102.5 6.4 %copy.58 = bf16[1,1,1024,2048]{3,2,1,0:T(8,128)(2,1)} copy(bf16[1,1,1024,2048]{2,3,1,0:T(8,128)(2,1)} %bitcast.35) | data formatting | bytes 8388608
  108.9 36.2 %all-to-all-done.2 = bf16[32,16,2048]{2,1,0:T(8,128)(2,1)S(1)} async-done(((bf16[32,16,2048]{2,1,0:T(8,128)(2,1)}), bf16[32,16,2048]{2,1,0:T(8,128)(2,1)S(1)}, u32[]{:S(2)}, u32[]{:S(2)}) %all-to-all-start.2) | async-done | bytes 2097184 | tf_op jit(solution)/shard_map/all_to_all | solution.py:54
  145.1 2.5 %copy.57 = bf16[512,2048]{0,1:T(8,128)(2,1)} copy(bf16[512,2048]{1,0:T(8,128)(2,1)S(1)} %bitcast.38) | data formatting | bytes 4194304 | tf_op jit(solution)/shard_map/reshape | solution.py:58
  147.6 3.0 %fusion.3 = bf16[256,8,256]{2,0,1:T(8,128)(2,1)S(1)} fusion(f32[32,8,8,256]{3,2,1,0:T(8,128)} %bitcast.41, bf16[8,256,512]{2,1,0:T(8,128)(2,1)} %bitcast.43, f32[256]{0:T(256)S(1)} %copy-done.2, f32[256,8]{0,1:T(8,128)S(1)} %add_sqrt_fusion, s32[256]{0:T(256)S(1)} %multiply_add_fusion), kind=kOutput, calls=%fused_computation.7 | convolution fusion | flops 540409856 | bytes 5253120 | tf_op jit(solution)/shard_map/dot_general | solution.py:56
  150.6 1.6 %copy.59 = bf16[256,8,256]{2,1,0:T(8,128)(2,1)} copy(bf16[256,8,256]{2,0,1:T(8,128)(2,1)S(1)} %fusion.3) | data formatting | bytes 2097152
  (10 shorter events, 0.1 us)
Async XLA Ops:
  0.6 94.4 %copy-start = (bf16[256,2560]{1,0:T(8,128)(2,1)S(1)}, bf16[256,2560]{1,0:T(8,128)(2,1)}, u32[]{:S(2)}) copy-start(bf16[256,2560]{1,0:T(8,128)(2,1)} %param.7) | copy-start | bytes 3932164
  2.5 17.4 %all-to-all-start.1 = ((s32[32,1,16]{2,1,0:T(1,128)}), s32[32,1,16]{2,1,0:T(1,128)S(1)}, u32[]{:S(2)}, u32[]{:S(2)}) async-start(s32[32,1,16]{2,1,0:T(1,128)} %bitcast.6), calls=%async_computation.1 | async-start | bytes 32768 | tf_op jit(solution)/shard_map/all_to_all | solution.py:49
  19.9 53.0 %all-to-all-start = ((bf16[2,4096,256]{2,0,1:T(2,128)(2,1)}), bf16[2,4096,256]{2,0,1:T(2,128)(2,1)}, u32[]{:S(2)}, u32[]{:S(2)}) async-start(bf16[2,4096,256]{2,0,1:T(2,128)(2,1)} %copy.49), calls=%async_computation | async-start | bytes 8388608 | tf_op jit(solution)/shard_map/all_to_all | solution.py:31
  90.3 54.8 %all-to-all-start.2 = ((bf16[32,16,2048]{2,1,0:T(8,128)(2,1)}), bf16[32,16,2048]{2,1,0:T(8,128)(2,1)S(1)}, u32[]{:S(2)}, u32[]{:S(2)}) async-start(bf16[32,16,2048]{2,1,0:T(8,128)(2,1)} %bitcast.42), calls=%async_computation.2 | async-start | bytes 4194304 | tf_op jit(solution)/shard_map/all_to_all | solution.py:54
  100.7 1.4 copy-start.1
  145.1 2.5 %copy-start.2 = (f32[256]{0:T(256)S(1)}, f32[256]{0:T(256)}, u32[]{:S(2)}) copy-start(f32[256]{0:T(256)} %param.9) | copy-start | bytes 3076
where the time goes:
time: 153 us; the launch traced here: 152 us
  waiting for transfers between devices  84.1 us (55%)
  local copies, waits for them, and re-layouts  34.3 us (22%)
  starting transfers between devices  16.9 us (11%)
  matrix products  14.5 us (9%)
  other arithmetic  1.55 us (1%)
    all_to_all x1, waiting for transfers between devices, on_device(): lax.all_to_all(table, 'grp', split_axis=1, concat_axis=0, tiled=True)  48 us
    all_to_all x1, waiting for transfers between devices, on_device(): lax.all_to_all(found, ('grp', 'dev'), split_axis=0, concat_axis=0, tiled=...  36.2 us
    unnamed x10, local copies, waits for them, and re-layouts  19.5 us
    all_to_all x1, starting transfers between devices, on_device(): lax.all_to_all(outgoing.reshape(peers, capacity), ('grp', 'dev'), split_a...  7.33 us
    transpose x1, local copies, waits for them, and re-layouts, on_device(): jnp.transpose(moved, (1, 0, 2)).reshape(row_count, layers * width)  6.44 us
    dot_general x1, matrix products, one_block(): jnp.dot(onehot, local_rows, preferred_element_type=jnp.float32)  5.91 us
    dot_general x1, matrix products, on_device(): jnp.dot(hidden, w_proj, preferred_element_type=jnp.float32)  5.61 us
    all_to_all x2, local copies, waits for them, and re-layouts, on_device(): lax.all_to_all(table, 'grp', split_axis=1, concat_axis=0, tiled=True)  5.05 us
  transfers between devices with their start and end apart: 3, of which 2 were waited for; matrix products, arithmetic and copies ran while one was open for 15% of the time, Pallas kernels for 0%

commit v1 on v0

--- a/solution.py
+++ b/solution.py
@@ -28,7 +28,10 @@
     layer_share, vocab_share, width = table.shape
     layers = layer_share * n_grp
     tok_count = token_ids.shape[0]
-    moved = lax.all_to_all(table, "grp", split_axis=1, concat_axis=0, tiled=True)
+    current_value = lax.axis_size("grp")
+    front = jnp.split(table, current_value, axis=1)
+    w1 = jnp.stack(front, axis=0)
+    moved = jnp.concatenate(lax.all_to_all(w1, "grp", 0, 0), axis=0)
     row_count = moved.shape[1]
     served_rows = jnp.transpose(moved, (1, 0, 2)).reshape(row_count, layers * width)
     served_table = served_rows.reshape(1, 1, row_count, layers * width)

time: 153 us -> 136 us (0.89)
  local copies, waits for them, and re-layouts: 34.3 us -> 25.4 us
  waiting for transfers between devices: 84.1 us -> 78.6 us
  other arithmetic: 1.55 us -> 3.85 us
  matrix products: 14.5 us -> 12.4 us
  starting transfers between devices: 16.9 us -> 15 us
    unnamed x10 -> x9, local copies, waits for them, and re-layouts: 19.5 us -> 5.7 us
    another operation x0 -> x2, local copies, waits for them, and re-layouts: none -> 9.82 us  [the longest x1 7.37 us: on_device(): served_table = served_rows.reshape(1, 1, row_count, layers * width)]
    all_to_all x1, waiting for transfers between devices: 36.2 us -> 28.7 us  [on_device(): lax.all_to_all(found, ('grp', 'dev'), split_axis=0, concat_axis=0, tiled=...]
    reshape x0 -> x1, local copies, waits for them, and re-layouts: none -> 6.55 us  [on_device(): moved = jnp.concatenate(lax.all_to_all(w1, 'grp', 0, 0), axis=0)]
    transpose x1 -> x0, local copies, waits for them, and re-layouts: 6.44 us -> none  [on_device(): jnp.transpose(moved, (1, 0, 2)).reshape(row_count, layers * width)]
    all_to_all x2 -> x0, local copies, waits for them, and re-layouts: 5.05 us -> none  [on_device(): lax.all_to_all(table, 'grp', split_axis=1, concat_axis=0, tiled=True)]
    all_to_all x1, waiting for transfers between devices: 0.01 us -> 2.34 us  [on_device(): lax.all_to_all(outgoing.reshape(peers, capacity), ('grp', 'dev'), split_a...]
    another operation x0 -> x1, other arithmetic: none -> 2.29 us  [on_device(): w1 = jnp.stack(front, axis=0)]
  transfers between devices with their start and end apart: 3 -> 3, of which waited for: 2 -> 3; matrix products, arithmetic and copies ran while one was open for 15% -> 19% of each run, Pallas kernels for 0% -> 0%
where the time goes in v1:
time: 136 us
  waiting for transfers between devices  78.6 us (58%)
  local copies, waits for them, and re-layouts  25.4 us (19%)
  starting transfers between devices  15 us (11%)
  matrix products  12.4 us (9%)
  other arithmetic  3.85 us (3%)
    all_to_all x1, waiting for transfers between devices, on_device(): moved = jnp.concatenate(lax.all_to_all(w1, 'grp', 0, 0), axis=0)  47.6 us
    all_to_all x1, waiting for transfers between devices, on_device(): lax.all_to_all(found, ('grp', 'dev'), split_axis=0, concat_axis=0, tiled=...  28.7 us
    another operation x1, local copies, waits for them, and re-layouts, on_device(): served_table = served_rows.reshape(1, 1, row_count, layers * width)  7.37 us
    all_to_all x1, starting transfers between devices, on_device(): lax.all_to_all(outgoing.reshape(peers, capacity), ('grp', 'dev'), split_a...  7.33 us
    reshape x1, local copies, waits for them, and re-layouts, on_device(): moved = jnp.concatenate(lax.all_to_all(w1, 'grp', 0, 0), axis=0)  6.55 us
    unnamed x9, local copies, waits for them, and re-layouts  5.7 us
    dot_general x1, matrix products, on_device(): jnp.dot(hidden, w_proj, preferred_element_type=jnp.float32)  5.61 us
    all_to_all x1, starting transfers between devices, on_device(): moved = jnp.concatenate(lax.all_to_all(w1, 'grp', 0, 0), axis=0)  4.86 us
  transfers between devices with their start and end apart: 3, of which 3 were waited for; matrix products, arithmetic and copies ran while one was open for 19% of the time, Pallas kernels for 0%

profile of v1, /device:TPU:0, one launch (start us, length us, event | category | flops | bytes accessed | tf_op | source)
XLA Modules:
  0.0 135.9 jit_solution(8997673052443607289)
XLA Ops:
  0.6 0.8 fusion.10
  1.4 0.2 convert_reduce_fusion
  1.6 0.2 select_reduce_fusion
  1.8 0.7 sub.35
  2.5 7.3 %all-to-all-start.1 = ((s32[32,1,16]{2,1,0:T(1,128)}), s32[32,1,16]{2,1,0:T(1,128)S(1)}, u32[]{:S(2)}, u32[]{:S(2)}) async-start(s32[32,1,16]{2,1,0:T(1,128)} %bitcast.7), calls=%async_computation.1 | async-start | bytes 32768 | tf_op jit(solution)/shard_map/all_to_all | solution.py:52
  9.8 2.5 %slice_bitcast_fusion.3 = (bf16[1,2,1024,256]{3,2,1,0:T(8,128)(2,1)S(1)}, bf16[1,2,1024,256]{3,2,1,0:T(8,128)(2,1)S(1)}, bf16[1,2,1024,256]{3,2,1,0:T(8,128)(2,1)S(1)}, bf16[1,2,1024,256]{3,2,1,0:T(8,128)(2,1)S(1)}) fusion(bf16[2,4096,256]{2,1,0:T(8,128)(2,1)} %param.5), kind=kLoop, calls=%fused_computation.13 | loop fusion | bytes 8388608 | tf_op jit(solution)/shard_map/stack | solution.py:33
  12.3 2.3 %pad_maximum_fusion = bf16[4,2,1024,256]{3,2,1,0:T(8,128)(2,1)} fusion(bf16[1,2,1024,256]{3,2,1,0:T(8,128)(2,1)S(1)} %get-tuple-element.29, bf16[1,2,1024,256]{3,2,1,0:T(8,128)(2,1)S(1)} %get-tuple-element.30, bf16[1,2,1024,256]{3,2,1,0:T(8,128)(2,1)S(1)} %get-tuple-element.28, bf16[1,2,1024,256]{3,2,1,0:T(8,128)(2,1)S(1)} %get-tuple-element.27), kind=kLoop, calls=%fused_computation | loop fusion | flops 6291456 | bytes 8388608 | tf_op jit(solution)/shard_map/stack | solution.py:33
  14.6 2.3 %all-to-all-done.1 = s32[32,1,16]{2,1,0:T(1,128)S(1)} async-done(((s32[32,1,16]{2,1,0:T(1,128)}), s32[32,1,16]{2,1,0:T(1,128)S(1)}, u32[]{:S(2)}, u32[]{:S(2)}) %all-to-all-start.1) | async-done | bytes 2080 | tf_op jit(solution)/shard_map/all_to_all | solution.py:52
  16.9 4.9 %all-to-all-start = ((bf16[4,2,1024,256]{3,2,1,0:T(8,128)(2,1)}), bf16[4,2,1024,256]{3,2,1,0:T(8,128)(2,1)}, u32[]{:S(2)}, u32[]{:S(2)}) async-start(bf16[4,2,1024,256]{3,2,1,0:T(8,128)(2,1)} %pad_maximum_fusion), calls=%async_computation | async-start | bytes 8388608 | tf_op jit(solution)/shard_map/all_to_all | solution.py:34
  21.9 0.1 sub.38
  21.9 47.6 %all-to-all-done = bf16[4,2,1024,256]{3,2,1,0:T(8,128)(2,1)} async-done(((bf16[4,2,1024,256]{3,2,1,0:T(8,128)(2,1)}), bf16[4,2,1024,256]{3,2,1,0:T(8,128)(2,1)}, u32[]{:S(2)}, u32[]{:S(2)}) %all-to-all-start) | async-done | bytes 4194336 | tf_op jit(solution)/shard_map/all_to_all | solution.py:34
  69.5 2.8 %copy.35 = bf16[128,8,8,256]{3,1,2,0:T(8,128)(2,1)S(1)} copy(bf16[128,8,8,256]{3,1,0,2:T(8,128)(2,1)} %bitcast.35) | data formatting | bytes 8388608
  72.3 3.7 %convolution_convert_fusion = bf16[512,2048]{1,0:T(8,128)(2,1)} fusion(bf16[1024,2048]{1,0:T(8,128)(2,1)S(1)} %bitcast.45, s32[512]{0:T(512)S(1)} %sub.38), kind=kOutput, calls=%fused_computation.1 | convolution fusion | flops 2149056512 | bytes 6293504 | tf_op jit(solution)/shard_map/while/body/eval_jaxpr/dot_general | solution.py:18
  76.0 2.8 %all-to-all-start.2 = ((bf16[32,16,2048]{2,1,0:T(8,128)(2,1)}), bf16[32,16,2048]{2,1,0:T(8,128)(2,1)S(1)}, u32[]{:S(2)}, u32[]{:S(2)}) async-start(bf16[32,16,2048]{2,1,0:T(8,128)(2,1)} %bitcast.48), calls=%async_computation.2 | async-start | bytes 4194304 | tf_op jit(solution)/shard_map/all_to_all | solution.py:57
  78.8 5.6 %fusion.11 = f32[256,2048]{1,0:T(8,128)S(1)} fusion(bf16[256,2560]{1,0:T(8,128)(2,1)S(1)} %copy-done, bf16[2560,2048]{1,0:T(8,128)(2,1)} %param.8), kind=kOutput, calls=%fused_computation.39 | convolution fusion | flops 2684354560 | bytes 13893632 | tf_op jit(solution)/shard_map/dot_general | solution.py:64
  84.5 0.9 copy.34
  85.3 0.5 copy-done.1
  85.8 0.3 multiply_reduce_fusion
  86.3 6.5 %copy.41 = bf16[8,1024,256]{2,0,1:T(8,128)(2,1)} copy(bf16[8,1024,256]{2,1,0:T(8,128)(2,1)} %bitcast.4) | data formatting | bytes 8388608 | tf_op jit(solution)/shard_map/reshape | solution.py:34
  92.8 7.4 %reshape_reshape.7 = bf16[1,1,1024,2048]{3,2,1,0:T(8,128)(2,1)} reshape(bf16[1024,8,256]{2,1,0:T(8,128)(2,1)} %bitcast.42) | data formatting | bytes 8388608 | tf_op jit(solution)/shard_map/reshape;reshape | solution.py:37
  100.2 28.7 %all-to-all-done.2 = bf16[32,16,2048]{2,1,0:T(8,128)(2,1)S(1)} async-done(((bf16[32,16,2048]{2,1,0:T(8,128)(2,1)}), bf16[32,16,2048]{2,1,0:T(8,128)(2,1)S(1)}, u32[]{:S(2)}, u32[]{:S(2)}) %all-to-all-start.2) | async-done | bytes 2097184 | tf_op jit(solution)/shard_map/all_to_all | solution.py:57
  128.9 2.5 %copy.31 = bf16[512,2048]{0,1:T(8,128)(2,1)} copy(bf16[512,2048]{1,0:T(8,128)(2,1)S(1)} %bitcast.43) | data formatting | bytes 4194304 | tf_op jit(solution)/shard_map/reshape | solution.py:61
  131.4 3.0 %fusion.3 = bf16[256,8,256]{2,0,1:T(8,128)(2,1)S(1)} fusion(f32[32,8,8,256]{3,2,1,0:T(8,128)} %bitcast.47, bf16[8,256,512]{2,1,0:T(8,128)(2,1)} %bitcast.49, f32[256]{0:T(256)S(1)} %copy-done.2, f32[256,8]{0,1:T(8,128)S(1)} %add_sqrt_fusion, s32[256]{0:T(256)S(1)} %multiply_add_fusion), kind=kOutput, calls=%fused_computation.8 | convolution fusion | flops 540409856 | bytes 5253120 | tf_op jit(solution)/shard_map/dot_general | solution.py:59
  134.4 1.6 %copy.32 = bf16[256,8,256]{2,1,0:T(8,128)(2,1)} copy(bf16[256,8,256]{2,0,1:T(8,128)(2,1)S(1)} %fusion.3) | data formatting | bytes 2097152
  (10 shorter events, 0.1 us)
Async XLA Ops:
  0.6 78.2 %copy-start = (bf16[256,2560]{1,0:T(8,128)(2,1)S(1)}, bf16[256,2560]{1,0:T(8,128)(2,1)}, u32[]{:S(2)}) copy-start(bf16[256,2560]{1,0:T(8,128)(2,1)} %param.7) | copy-start | bytes 3932164
  2.5 14.4 %all-to-all-start.1 = ((s32[32,1,16]{2,1,0:T(1,128)}), s32[32,1,16]{2,1,0:T(1,128)S(1)}, u32[]{:S(2)}, u32[]{:S(2)}) async-start(s32[32,1,16]{2,1,0:T(1,128)} %bitcast.7), calls=%async_computation.1 | async-start | bytes 32768 | tf_op jit(solution)/shard_map/all_to_all | solution.py:52
  16.9 52.6 %all-to-all-start = ((bf16[4,2,1024,256]{3,2,1,0:T(8,128)(2,1)}), bf16[4,2,1024,256]{3,2,1,0:T(8,128)(2,1)}, u32[]{:S(2)}, u32[]{:S(2)}) async-start(bf16[4,2,1024,256]{3,2,1,0:T(8,128)(2,1)} %pad_maximum_fusion), calls=%async_computation | async-start | bytes 8388608 | tf_op jit(solution)/shard_map/all_to_all | solution.py:34
  76.0 52.8 %all-to-all-start.2 = ((bf16[32,16,2048]{2,1,0:T(8,128)(2,1)}), bf16[32,16,2048]{2,1,0:T(8,128)(2,1)S(1)}, u32[]{:S(2)}, u32[]{:S(2)}) async-start(bf16[32,16,2048]{2,1,0:T(8,128)(2,1)} %bitcast.48), calls=%async_computation.2 | async-start | bytes 4194304 | tf_op jit(solution)/shard_map/all_to_all | solution.py:57
  84.4 1.4 %copy-start.1 = (f32[256,2048]{1,0:T(8,128)}, f32[256,2048]{1,0:T(8,128)S(1)}, u32[]{:S(2)}) copy-start(f32[256,2048]{1,0:T(8,128)S(1)} %fusion.11) | copy-start | bytes 6291460
  128.8 2.5 %copy-start.2 = (f32[256]{0:T(256)S(1)}, f32[256]{0:T(256)}, u32[]{:S(2)}) copy-start(f32[256]{0:T(256)} %param.9) | copy-start | bytes 3076
